TPU v7x, 32 devices: a 4x2x2 block of a 4x4x8 slice. The times are simulated.
32 devices in a mesh: data: 4 (over y, z), group: 8 (over x, core).
Axes of the slice: x: 4, y: 2, z: 2, core: 2. Of those that a mesh axis runs over, the one named last changes fastest.
The devices are a block of a 4x4x8 slice.
Arguments:
- latents: bfloat16 [4096, 384], P(('data', 'group')), parts along dimension 0
- hint_embed: bfloat16 [4096, 384], P(('data', 'group')), parts along dimension 0
- in_qkv: bfloat16 [2, 17, 384, 1152], replicated
- in_proj: bfloat16 [2, 17, 6, 64, 384], replicated
- in_up: bfloat16 [2, 17, 384, 1536], replicated
- in_down: bfloat16 [2, 17, 1536, 384], replicated
- in_norm: bfloat16 [2, 17, 4, 384], replicated
- out_qkv: bfloat16 [16, 384, 1152], replicated
- out_proj: bfloat16 [16, 6, 64, 384], replicated
- out_up: bfloat16 [16, 384, 1536], replicated
- out_down: bfloat16 [16, 1536, 384], replicated
- out_norm: bfloat16 [16, 4, 384], replicated
- zero_proj: bfloat16 [17, 384, 384], replicated
- hint_proj: bfloat16 [384, 384], replicated
- skip_proj: bfloat16 [16, 768, 384], replicated
- final_norm: bfloat16 [2, 384], replicated
- w_out: bfloat16 [384, 384], replicated
Outputs:
- output: bfloat16 [4096, 384], P(('data', 'group')), parts along dimension 0
There are 4 independent parts. A program takes and returns all parts, laid end to end along the dimension named above; an argument that names none is the same for every part.
All inputs are finite; a program needn't handle non-finite values.
Results may differ from a plain program's by a relative error of at most 0.02.
Values are sent between devices in bfloat16 or wider.
A program may use at most 768 MiB of HBM per device.

v0:
```python
import jax
import jax.numpy as jnp
from jax import lax
from jax.sharding import PartitionSpec as P

EPS = 1e-6


def mat_f32(left_op, right_op):
    return jnp.dot(left_op, right_op, preferred_element_type=jnp.float32)


def layer_norm(values, norm_gain, norm_shift):
    wide_vals = values.astype(jnp.float32)
    centered = wide_vals - jnp.mean(wide_vals, axis=-1, keepdims=True)
    variance = jnp.mean(centered * centered, axis=-1, keepdims=True)
    normed = centered * lax.rsqrt(variance + EPS)
    return (normed * norm_gain.astype(jnp.float32) + norm_shift.astype(jnp.float32)).astype(jnp.bfloat16)


def gather_half(local_rows, half_size):
    gathered = local_rows
    offset_bit = 1
    while offset_bit < half_size:
        partner_perm = [(dev_id, dev_id ^ offset_bit) for dev_id in range(2 * half_size)]
        gathered = jnp.concatenate([gathered, lax.ppermute(gathered, "group", partner_perm)], axis=0)
        offset_bit = offset_bit * 2
    return gathered


def transformer_block(residual, w_qkv, w_proj, w_up, w_down, norm_rows, half_size):
    tok_count, model_width = residual.shape
    head_count, head_dim = w_proj.shape[0], w_proj.shape[1]
    normed = layer_norm(residual, norm_rows[0], norm_rows[1])
    qkv_all = mat_f32(normed, w_qkv).astype(jnp.bfloat16)
    queries = qkv_all[:, :model_width].reshape(tok_count, head_count, head_dim)
    key_vals = gather_half(qkv_all[:, model_width:], half_size)
    key_heads = key_vals[:, :model_width].reshape(-1, head_count, head_dim)
    val_heads = key_vals[:, model_width:].reshape(-1, head_count, head_dim)
    scores = jnp.einsum("thd,nhd->htn", queries, key_heads, preferred_element_type=jnp.float32) * head_dim ** -0.5
    att_probs = jax.nn.softmax(scores, axis=-1).astype(jnp.bfloat16)
    head_out = jnp.einsum("htn,nhd->thd", att_probs, val_heads, preferred_element_type=jnp.float32).astype(jnp.bfloat16)
    attn_sum = jnp.einsum("thd,hde->te", head_out, w_proj, preferred_element_type=jnp.float32)
    residual = (residual.astype(jnp.float32) + attn_sum).astype(jnp.bfloat16)
    normed = layer_norm(residual, norm_rows[2], norm_rows[3])
    hidden = jax.nn.gelu(mat_f32(normed, w_up), approximate=True).astype(jnp.bfloat16)
    return (residual.astype(jnp.float32) + mat_f32(hidden, w_down)).astype(jnp.bfloat16)


def solution(mesh):
    group_size = mesh.shape["group"]
    half_size = group_size // 2
    swap_perm = [(dev_id, (dev_id + half_size) % group_size) for dev_id in range(group_size)]
    to_base = [(dev_id + half_size, dev_id) for dev_id in range(half_size)]
    to_ctrl = [(dev_id, dev_id + half_size) for dev_id in range(half_size)]

    def device_step(x_own, hint_own, in_qkv, in_proj, in_up, in_down, in_norm, out_qkv, out_proj, out_up, out_down, out_norm, zero_proj, hint_proj, skip_proj, final_norm, w_out):
        layers = skip_proj.shape[0]
        tok_own, model_width = x_own.shape
        branch = lax.axis_index("group") // half_size
        is_base = branch == 0
        x_other = lax.ppermute(x_own, "group", swap_perm)
        hint_recv = lax.ppermute(hint_own, "group", to_ctrl)
        x_local = jnp.where(is_base, jnp.concatenate([x_own, x_other], axis=0), jnp.concatenate([x_other, x_own], axis=0))
        hint_local = jnp.where(is_base, jnp.zeros((2 * tok_own, model_width), jnp.bfloat16), jnp.concatenate([hint_recv, hint_own], axis=0))
        residual = (x_local.astype(jnp.float32) + mat_f32(hint_local, hint_proj)).astype(jnp.bfloat16)
        sum_list = []
        for layer_idx in range(layers + 1):
            residual = transformer_block(residual, in_qkv[branch, layer_idx], in_proj[branch, layer_idx], in_up[branch, layer_idx], in_down[branch, layer_idx], in_norm[branch, layer_idx], half_size)
            ctrl_res = mat_f32(residual, zero_proj[layer_idx]).astype(jnp.bfloat16)
            res_recv = lax.ppermute(ctrl_res, "group", to_base)
            sum_list.append((residual.astype(jnp.float32) + res_recv.astype(jnp.float32)).astype(jnp.bfloat16))
        out_state = sum_list.pop()
        for layer_idx in range(layers):
            skip_val = sum_list[layers - 1 - layer_idx]
            top_part = mat_f32(out_state, skip_proj[layer_idx, :model_width])
            low_part = mat_f32(skip_val, skip_proj[layer_idx, model_width:])
            merged = (top_part + low_part).astype(jnp.bfloat16)
            out_state = transformer_block(merged, out_qkv[layer_idx], out_proj[layer_idx], out_up[layer_idx], out_down[layer_idx], out_norm[layer_idx], half_size)
        normed = layer_norm(out_state, final_norm[0], final_norm[1])
        y_local = mat_f32(normed, w_out).astype(jnp.bfloat16)
        y_recv = lax.ppermute(y_local[tok_own:], "group", to_ctrl)
        return jnp.where(is_base, y_local[:tok_own], y_recv)

    tok_spec = P(("data", "group"), None)
    return jax.shard_map(device_step, mesh=mesh, in_specs=(tok_spec, tok_spec) + (P(),) * 15, out_specs=tok_spec, check_vma=False)
```

profile of v0, /device:TPU:86, one launch (start us, length us, event | category | flops | bytes accessed | tf_op | source)
XLA Modules:
  0.0 1335.1 jit_solution(7139347864480616671)
XLA Ops:
  15.1 19.0 %collective-permute-done.3 = bf16[512,768]{1,0:T(8,128)(2,1)S(1)} collective-permute-done((bf16[512,768]{1,0:T(8,128)(2,1)S(1)}, bf16[512,768]{1,0:T(8,128)(2,1)S(1)}, u32[]{:S(2)}, u32[]{:S(2)}) %collective-permute-start.3) | collective-permute-done | bytes 786464 | tf_op jit(solution)/shard_map/ppermute | solution.py:26
  53.4 19.0 %collective-permute-done.5 = bf16[512,768]{1,0:T(8,128)(2,1)S(1)} collective-permute-done((bf16[512,768]{1,0:T(8,128)(2,1)S(1)}, bf16[512,768]{1,0:T(8,128)(2,1)S(1)}, u32[]{:S(2)}, u32[]{:S(2)}) %collective-permute-start.5) | collective-permute-done | bytes 786464 | tf_op jit(solution)/shard_map/ppermute | solution.py:26
  92.0 19.0 %collective-permute-done.7 = bf16[512,768]{1,0:T(8,128)(2,1)S(1)} collective-permute-done((bf16[512,768]{1,0:T(8,128)(2,1)S(1)}, bf16[512,768]{1,0:T(8,128)(2,1)S(1)}, u32[]{:S(2)}, u32[]{:S(2)}) %collective-permute-start.7) | collective-permute-done | bytes 786464 | tf_op jit(solution)/shard_map/ppermute | solution.py:26
  130.4 19.0 %collective-permute-done.9 = bf16[512,768]{1,0:T(8,128)(2,1)S(1)} collective-permute-done((bf16[512,768]{1,0:T(8,128)(2,1)S(1)}, bf16[512,768]{1,0:T(8,128)(2,1)S(1)}, u32[]{:S(2)}, u32[]{:S(2)}) %collective-permute-start.9) | collective-permute-done | bytes 786464 | tf_op jit(solution)/shard_map/ppermute | solution.py:26
  168.9 19.0 %collective-permute-done.11 = bf16[512,768]{1,0:T(8,128)(2,1)S(1)} collective-permute-done((bf16[512,768]{1,0:T(8,128)(2,1)S(1)}, bf16[512,768]{1,0:T(8,128)(2,1)S(1)}, u32[]{:S(2)}, u32[]{:S(2)}) %collective-permute-start.11) | collective-permute-done | bytes 786464 | tf_op jit(solution)/shard_map/ppermute | solution.py:26
  207.3 19.0 %collective-permute-done.13 = bf16[512,768]{1,0:T(8,128)(2,1)S(1)} collective-permute-done((bf16[512,768]{1,0:T(8,128)(2,1)S(1)}, bf16[512,768]{1,0:T(8,128)(2,1)S(1)}, u32[]{:S(2)}, u32[]{:S(2)}) %collective-permute-start.13) | collective-permute-done | bytes 786464 | tf_op jit(solution)/shard_map/ppermute | solution.py:26
  246.1 19.0 %collective-permute-done.15 = bf16[512,768]{1,0:T(8,128)(2,1)S(1)} collective-permute-done((bf16[512,768]{1,0:T(8,128)(2,1)S(1)}, bf16[512,768]{1,0:T(8,128)(2,1)S(1)}, u32[]{:S(2)}, u32[]{:S(2)}) %collective-permute-start.15) | collective-permute-done | bytes 786464 | tf_op jit(solution)/shard_map/ppermute | solution.py:26
  284.4 19.0 %collective-permute-done.17 = bf16[512,768]{1,0:T(8,128)(2,1)S(1)} collective-permute-done((bf16[512,768]{1,0:T(8,128)(2,1)S(1)}, bf16[512,768]{1,0:T(8,128)(2,1)S(1)}, u32[]{:S(2)}, u32[]{:S(2)}) %collective-permute-start.17) | collective-permute-done | bytes 786464 | tf_op jit(solution)/shard_map/ppermute | solution.py:26
  323.0 19.0 %collective-permute-done.19 = bf16[512,768]{1,0:T(8,128)(2,1)S(1)} collective-permute-done((bf16[512,768]{1,0:T(8,128)(2,1)S(1)}, bf16[512,768]{1,0:T(8,128)(2,1)S(1)}, u32[]{:S(2)}, u32[]{:S(2)}) %collective-permute-start.19) | collective-permute-done | bytes 786464 | tf_op jit(solution)/shard_map/ppermute | solution.py:26
  361.4 19.0 %collective-permute-done.21 = bf16[512,768]{1,0:T(8,128)(2,1)S(1)} collective-permute-done((bf16[512,768]{1,0:T(8,128)(2,1)S(1)}, bf16[512,768]{1,0:T(8,128)(2,1)S(1)}, u32[]{:S(2)}, u32[]{:S(2)}) %collective-permute-start.21) | collective-permute-done | bytes 786464 | tf_op jit(solution)/shard_map/ppermute | solution.py:26
  399.9 19.0 %collective-permute-done.23 = bf16[512,768]{1,0:T(8,128)(2,1)S(1)} collective-permute-done((bf16[512,768]{1,0:T(8,128)(2,1)S(1)}, bf16[512,768]{1,0:T(8,128)(2,1)S(1)}, u32[]{:S(2)}, u32[]{:S(2)}) %collective-permute-start.23) | collective-permute-done | bytes 786464 | tf_op jit(solution)/shard_map/ppermute | solution.py:26
  438.3 19.0 %collective-permute-done.25 = bf16[512,768]{1,0:T(8,128)(2,1)S(1)} collective-permute-done((bf16[512,768]{1,0:T(8,128)(2,1)S(1)}, bf16[512,768]{1,0:T(8,128)(2,1)S(1)}, u32[]{:S(2)}, u32[]{:S(2)}) %collective-permute-start.25) | collective-permute-done | bytes 786464 | tf_op jit(solution)/shard_map/ppermute | solution.py:26
  477.2 19.0 %collective-permute-done.27 = bf16[512,768]{1,0:T(8,128)(2,1)S(1)} collective-permute-done((bf16[512,768]{1,0:T(8,128)(2,1)S(1)}, bf16[512,768]{1,0:T(8,128)(2,1)S(1)}, u32[]{:S(2)}, u32[]{:S(2)}) %collective-permute-start.27) | collective-permute-done | bytes 786464 | tf_op jit(solution)/shard_map/ppermute | solution.py:26
  515.6 19.0 %collective-permute-done.29 = bf16[512,768]{1,0:T(8,128)(2,1)S(1)} collective-permute-done((bf16[512,768]{1,0:T(8,128)(2,1)S(1)}, bf16[512,768]{1,0:T(8,128)(2,1)S(1)}, u32[]{:S(2)}, u32[]{:S(2)}) %collective-permute-start.29) | collective-permute-done | bytes 786464 | tf_op jit(solution)/shard_map/ppermute | solution.py:26
  554.9 18.4 %collective-permute-done.31 = bf16[512,768]{1,0:T(8,128)(2,1)S(1)} collective-permute-done((bf16[512,768]{1,0:T(8,128)(2,1)S(1)}, bf16[512,768]{1,0:T(8,128)(2,1)S(1)}, u32[]{:S(2)}, u32[]{:S(2)}) %collective-permute-start.31) | collective-permute-done | bytes 786464 | tf_op jit(solution)/shard_map/ppermute | solution.py:26
  592.7 19.0 %collective-permute-done.33 = bf16[512,768]{1,0:T(8,128)(2,1)} collective-permute-done((bf16[512,768]{1,0:T(8,128)(2,1)S(1)}, bf16[512,768]{1,0:T(8,128)(2,1)}, u32[]{:S(2)}, u32[]{:S(2)}) %collective-permute-start.33) | collective-permute-done | bytes 786464 | tf_op jit(solution)/shard_map/ppermute | solution.py:26
  636.0 16.3 %collective-permute-done.35 = bf16[512,768]{1,0:T(8,128)(2,1)} collective-permute-done((bf16[512,768]{1,0:T(8,128)(2,1)S(1)}, bf16[512,768]{1,0:T(8,128)(2,1)}, u32[]{:S(2)}, u32[]{:S(2)}) %collective-permute-start.35) | collective-permute-done | bytes 786464 | tf_op jit(solution)/shard_map/ppermute | solution.py:26
  732.1 11.9 collective-permute-done.42
  774.6 13.5 %collective-permute-done.45 = bf16[512,768]{1,0:T(8,128)(2,1)} collective-permute-done((bf16[512,768]{1,0:T(8,128)(2,1)S(1)}, bf16[512,768]{1,0:T(8,128)(2,1)}, u32[]{:S(2)}, u32[]{:S(2)}) %collective-permute-start.45) | collective-permute-done | bytes 786464 | tf_op jit(solution)/shard_map/ppermute | solution.py:26
  819.9 12.3 collective-permute-done.48
  858.6 13.7 %collective-permute-done.51 = bf16[512,768]{1,0:T(8,128)(2,1)S(1)} collective-permute-done((bf16[512,768]{1,0:T(8,128)(2,1)S(1)}, bf16[512,768]{1,0:T(8,128)(2,1)S(1)}, u32[]{:S(2)}, u32[]{:S(2)}) %collective-permute-start.51) | collective-permute-done | bytes 786464 | tf_op jit(solution)/shard_map/ppermute | solution.py:26
  898.1 14.3 %collective-permute-done.54 = bf16[512,768]{1,0:T(8,128)(2,1)S(1)} collective-permute-done((bf16[512,768]{1,0:T(8,128)(2,1)S(1)}, bf16[512,768]{1,0:T(8,128)(2,1)S(1)}, u32[]{:S(2)}, u32[]{:S(2)}) %collective-permute-start.54) | collective-permute-done | bytes 786464 | tf_op jit(solution)/shard_map/ppermute | solution.py:26
  937.6 14.9 %collective-permute-done.57 = bf16[512,768]{1,0:T(8,128)(2,1)S(1)} collective-permute-done((bf16[512,768]{1,0:T(8,128)(2,1)S(1)}, bf16[512,768]{1,0:T(8,128)(2,1)S(1)}, u32[]{:S(2)}, u32[]{:S(2)}) %collective-permute-start.57) | collective-permute-done | bytes 786464 | tf_op jit(solution)/shard_map/ppermute | solution.py:26
  976.9 15.7 %collective-permute-done.60 = bf16[512,768]{1,0:T(8,128)(2,1)S(1)} collective-permute-done((bf16[512,768]{1,0:T(8,128)(2,1)S(1)}, bf16[512,768]{1,0:T(8,128)(2,1)S(1)}, u32[]{:S(2)}, u32[]{:S(2)}) %collective-permute-start.60) | collective-permute-done | bytes 786464 | tf_op jit(solution)/shard_map/ppermute | solution.py:26
  1017.0 15.7 %collective-permute-done.63 = bf16[512,768]{1,0:T(8,128)(2,1)S(1)} collective-permute-done((bf16[512,768]{1,0:T(8,128)(2,1)S(1)}, bf16[512,768]{1,0:T(8,128)(2,1)S(1)}, u32[]{:S(2)}, u32[]{:S(2)}) %collective-permute-start.63) | collective-permute-done | bytes 786464 | tf_op jit(solution)/shard_map/ppermute | solution.py:26
  1057.1 15.6 %collective-permute-done.66 = bf16[512,768]{1,0:T(8,128)(2,1)S(1)} collective-permute-done((bf16[512,768]{1,0:T(8,128)(2,1)S(1)}, bf16[512,768]{1,0:T(8,128)(2,1)S(1)}, u32[]{:S(2)}, u32[]{:S(2)}) %collective-permute-start.66) | collective-permute-done | bytes 786464 | tf_op jit(solution)/shard_map/ppermute | solution.py:26
  1097.6 15.3 %collective-permute-done.69 = bf16[512,768]{1,0:T(8,128)(2,1)S(1)} collective-permute-done((bf16[512,768]{1,0:T(8,128)(2,1)S(1)}, bf16[512,768]{1,0:T(8,128)(2,1)S(1)}, u32[]{:S(2)}, u32[]{:S(2)}) %collective-permute-start.69) | collective-permute-done | bytes 786464 | tf_op jit(solution)/shard_map/ppermute | solution.py:26
  1137.2 15.8 %collective-permute-done.72 = bf16[512,768]{1,0:T(8,128)(2,1)S(1)} collective-permute-done((bf16[512,768]{1,0:T(8,128)(2,1)S(1)}, bf16[512,768]{1,0:T(8,128)(2,1)S(1)}, u32[]{:S(2)}, u32[]{:S(2)}) %collective-permute-start.72) | collective-permute-done | bytes 786464 | tf_op jit(solution)/shard_map/ppermute | solution.py:26
  1177.3 15.7 %collective-permute-done.75 = bf16[512,768]{1,0:T(8,128)(2,1)S(1)} collective-permute-done((bf16[512,768]{1,0:T(8,128)(2,1)S(1)}, bf16[512,768]{1,0:T(8,128)(2,1)S(1)}, u32[]{:S(2)}, u32[]{:S(2)}) %collective-permute-start.75) | collective-permute-done | bytes 786464 | tf_op jit(solution)/shard_map/ppermute | solution.py:26
  1217.4 15.7 %collective-permute-done.78 = bf16[512,768]{1,0:T(8,128)(2,1)S(1)} collective-permute-done((bf16[512,768]{1,0:T(8,128)(2,1)S(1)}, bf16[512,768]{1,0:T(8,128)(2,1)S(1)}, u32[]{:S(2)}, u32[]{:S(2)}) %collective-permute-start.78) | collective-permute-done | bytes 786464 | tf_op jit(solution)/shard_map/ppermute | solution.py:26
  1257.5 15.6 %collective-permute-done.81 = bf16[512,768]{1,0:T(8,128)(2,1)S(1)} collective-permute-done((bf16[512,768]{1,0:T(8,128)(2,1)S(1)}, bf16[512,768]{1,0:T(8,128)(2,1)S(1)}, u32[]{:S(2)}, u32[]{:S(2)}) %collective-permute-start.81) | collective-permute-done | bytes 786464 | tf_op jit(solution)/shard_map/ppermute | solution.py:26
  1293.4 19.0 %collective-permute-done.84 = bf16[512,768]{1,0:T(8,128)(2,1)S(1)} collective-permute-done((bf16[512,768]{1,0:T(8,128)(2,1)S(1)}, bf16[512,768]{1,0:T(8,128)(2,1)S(1)}, u32[]{:S(2)}, u32[]{:S(2)}) %collective-permute-start.84) | collective-permute-done | bytes 786464 | tf_op jit(solution)/shard_map/ppermute | solution.py:26
  (928 shorter events, 786.1 us)
Async XLA Ops:
  631.8 20.5 %collective-permute-start.35 = (bf16[512,768]{1,0:T(8,128)(2,1)S(1)}, bf16[512,768]{1,0:T(8,128)(2,1)}, u32[]{:S(2)}, u32[]{:S(2)}) collective-permute-start(bf16[512,768]{1,0:T(8,128)(2,1)S(1)} %pad_maximum_fusion.49), channel_id=1, source_target_pairs={{0,2},{1,3},{2,0},{3,1},{4,6},{5,7},{6,4},{7,5},{8,10},{9,11},{10,... | collective-permute-start | bytes 2359304 | tf_op jit(solution)/shard_map/ppermute | solution.py:26
  633.8 37.5 %collective-permute-start.37 = (bf16[256,384]{1,0:T(8,128)(2,1)S(1)}, bf16[256,384]{1,0:T(8,128)(2,1)S(1)}, u32[]{:S(2)}, u32[]{:S(2)}) collective-permute-start(bf16[256,384]{1,0:T(8,128)(2,1)S(1)} %convolution_convert_fusion.49), channel_id=1, source_target_pairs={{4,0},{5,1},{6,2},{7,3},{12,8},{13,9},{14,10},{15,11},{20,16},{21,... | collective-permute-start | bytes 589832 | tf_op jit(solution)/shard_map/ppermute | solution.py:71
  679.3 20.5 %collective-permute-start.39 = (bf16[512,768]{1,0:T(8,128)(2,1)S(1)}, bf16[512,768]{1,0:T(8,128)(2,1)}, u32[]{:S(2)}, u32[]{:S(2)}) collective-permute-start(bf16[512,768]{1,0:T(8,128)(2,1)S(1)} %pad_maximum_fusion.50), channel_id=1, source_target_pairs={{0,2},{1,3},{2,0},{3,1},{4,6},{5,7},{6,4},{7,5},{8,10},{9,11},{10,... | collective-permute-start | bytes 2359304 | tf_op jit(solution)/shard_map/ppermute | solution.py:26
  681.7 36.5 %collective-permute-start.40 = (bf16[256,384]{1,0:T(8,128)(2,1)}, bf16[256,384]{1,0:T(8,128)(2,1)S(1)}, u32[]{:S(2)}, u32[]{:S(2)}) collective-permute-start(bf16[256,384]{1,0:T(8,128)(2,1)} %convolution_convert_fusion.48), channel_id=1, source_target_pairs={{4,0},{5,1},{6,2},{7,3},{12,8},{13,9},{14,10},{15,11},{20,16},{21,... | collective-permute-start | bytes 589832 | tf_op jit(solution)/shard_map/ppermute | solution.py:71
  723.5 20.5 %collective-permute-start.42 = (bf16[512,768]{1,0:T(8,128)(2,1)S(1)}, bf16[512,768]{1,0:T(8,128)(2,1)}, u32[]{:S(2)}, u32[]{:S(2)}) collective-permute-start(bf16[512,768]{1,0:T(8,128)(2,1)S(1)} %pad_maximum_fusion.51), channel_id=1, source_target_pairs={{0,2},{1,3},{2,0},{3,1},{4,6},{5,7},{6,4},{7,5},{8,10},{9,11},{10,... | collective-permute-start | bytes 2359304 | tf_op jit(solution)/shard_map/ppermute | solution.py:26
  726.0 36.4 %collective-permute-start.43 = (bf16[256,384]{1,0:T(8,128)(2,1)}, bf16[256,384]{1,0:T(8,128)(2,1)S(1)}, u32[]{:S(2)}, u32[]{:S(2)}) collective-permute-start(bf16[256,384]{1,0:T(8,128)(2,1)} %convolution_convert_fusion.47), channel_id=1, source_target_pairs={{4,0},{5,1},{6,2},{7,3},{12,8},{13,9},{14,10},{15,11},{20,16},{21,... | collective-permute-start | bytes 589832 | tf_op jit(solution)/shard_map/ppermute | solution.py:71
  767.6 20.5 %collective-permute-start.45 = (bf16[512,768]{1,0:T(8,128)(2,1)S(1)}, bf16[512,768]{1,0:T(8,128)(2,1)}, u32[]{:S(2)}, u32[]{:S(2)}) collective-permute-start(bf16[512,768]{1,0:T(8,128)(2,1)S(1)} %pad_maximum_fusion.52), channel_id=1, source_target_pairs={{0,2},{1,3},{2,0},{3,1},{4,6},{5,7},{6,4},{7,5},{8,10},{9,11},{10,... | collective-permute-start | bytes 2359304 | tf_op jit(solution)/shard_map/ppermute | solution.py:26
  769.3 37.2 %collective-permute-start.46 = (bf16[256,384]{1,0:T(8,128)(2,1)S(1)}, bf16[256,384]{1,0:T(8,128)(2,1)S(1)}, u32[]{:S(2)}, u32[]{:S(2)}) collective-permute-start(bf16[256,384]{1,0:T(8,128)(2,1)S(1)} %convolution_convert_fusion.46), channel_id=1, source_target_pairs={{4,0},{5,1},{6,2},{7,3},{12,8},{13,9},{14,10},{15,11},{20,16},{21,... | collective-permute-start | bytes 589832 | tf_op jit(solution)/shard_map/ppermute | solution.py:71
  811.7 20.5 %collective-permute-start.48 = (bf16[512,768]{1,0:T(8,128)(2,1)S(1)}, bf16[512,768]{1,0:T(8,128)(2,1)S(1)}, u32[]{:S(2)}, u32[]{:S(2)}) collective-permute-start(bf16[512,768]{1,0:T(8,128)(2,1)S(1)} %pad_maximum_fusion.53), channel_id=1, source_target_pairs={{0,2},{1,3},{2,0},{3,1},{4,6},{5,7},{6,4},{7,5},{8,10},{9,11},{10,... | collective-permute-start | bytes 2359304 | tf_op jit(solution)/shard_map/ppermute | solution.py:26
  814.1 32.4 %collective-permute-start.49 = (bf16[256,384]{1,0:T(8,128)(2,1)}, bf16[256,384]{1,0:T(8,128)(2,1)}, u32[]{:S(2)}, u32[]{:S(2)}) collective-permute-start(bf16[256,384]{1,0:T(8,128)(2,1)} %convolution_convert_fusion.45), channel_id=1, source_target_pairs={{4,0},{5,1},{6,2},{7,3},{12,8},{13,9},{14,10},{15,11},{20,16},{21,... | collective-permute-start | bytes 589832 | tf_op jit(solution)/shard_map/ppermute | solution.py:71
  851.8 20.5 %collective-permute-start.51 = (bf16[512,768]{1,0:T(8,128)(2,1)S(1)}, bf16[512,768]{1,0:T(8,128)(2,1)S(1)}, u32[]{:S(2)}, u32[]{:S(2)}) collective-permute-start(bf16[512,768]{1,0:T(8,128)(2,1)S(1)} %pad_maximum_fusion.54), channel_id=1, source_target_pairs={{0,2},{1,3},{2,0},{3,1},{4,6},{5,7},{6,4},{7,5},{8,10},{9,11},{10,... | collective-permute-start | bytes 2359304 | tf_op jit(solution)/shard_map/ppermute | solution.py:26
  854.3 32.4 %collective-permute-start.52 = (bf16[256,384]{1,0:T(8,128)(2,1)}, bf16[256,384]{1,0:T(8,128)(2,1)S(1)}, u32[]{:S(2)}, u32[]{:S(2)}) collective-permute-start(bf16[256,384]{1,0:T(8,128)(2,1)} %convolution_convert_fusion.44), channel_id=1, source_target_pairs={{4,0},{5,1},{6,2},{7,3},{12,8},{13,9},{14,10},{15,11},{20,16},{21,... | collective-permute-start | bytes 589832 | tf_op jit(solution)/shard_map/ppermute | solution.py:71
  891.9 20.5 %collective-permute-start.54 = (bf16[512,768]{1,0:T(8,128)(2,1)S(1)}, bf16[512,768]{1,0:T(8,128)(2,1)S(1)}, u32[]{:S(2)}, u32[]{:S(2)}) collective-permute-start(bf16[512,768]{1,0:T(8,128)(2,1)S(1)} %pad_maximum_fusion.55), channel_id=1, source_target_pairs={{0,2},{1,3},{2,0},{3,1},{4,6},{5,7},{6,4},{7,5},{8,10},{9,11},{10,... | collective-permute-start | bytes 2359304 | tf_op jit(solution)/shard_map/ppermute | solution.py:26
  894.3 32.4 %collective-permute-start.55 = (bf16[256,384]{1,0:T(8,128)(2,1)}, bf16[256,384]{1,0:T(8,128)(2,1)S(1)}, u32[]{:S(2)}, u32[]{:S(2)}) collective-permute-start(bf16[256,384]{1,0:T(8,128)(2,1)} %convolution_convert_fusion.43), channel_id=1, source_target_pairs={{4,0},{5,1},{6,2},{7,3},{12,8},{13,9},{14,10},{15,11},{20,16},{21,... | collective-permute-start | bytes 589832 | tf_op jit(solution)/shard_map/ppermute | solution.py:71
  932.0 20.5 %collective-permute-start.57 = (bf16[512,768]{1,0:T(8,128)(2,1)S(1)}, bf16[512,768]{1,0:T(8,128)(2,1)S(1)}, u32[]{:S(2)}, u32[]{:S(2)}) collective-permute-start(bf16[512,768]{1,0:T(8,128)(2,1)S(1)} %pad_maximum_fusion.56), channel_id=1, source_target_pairs={{0,2},{1,3},{2,0},{3,1},{4,6},{5,7},{6,4},{7,5},{8,10},{9,11},{10,... | collective-permute-start | bytes 2359304 | tf_op jit(solution)/shard_map/ppermute | solution.py:26
  935.0 31.8 %collective-permute-start.58 = (bf16[256,384]{1,0:T(8,128)(2,1)}, bf16[256,384]{1,0:T(8,128)(2,1)S(1)}, u32[]{:S(2)}, u32[]{:S(2)}) collective-permute-start(bf16[256,384]{1,0:T(8,128)(2,1)} %convolution_convert_fusion.42), channel_id=1, source_target_pairs={{4,0},{5,1},{6,2},{7,3},{12,8},{13,9},{14,10},{15,11},{20,16},{21,... | collective-permute-start | bytes 589832 | tf_op jit(solution)/shard_map/ppermute | solution.py:71
  972.1 20.5 %collective-permute-start.60 = (bf16[512,768]{1,0:T(8,128)(2,1)S(1)}, bf16[512,768]{1,0:T(8,128)(2,1)S(1)}, u32[]{:S(2)}, u32[]{:S(2)}) collective-permute-start(bf16[512,768]{1,0:T(8,128)(2,1)S(1)} %pad_maximum_fusion.57), channel_id=1, source_target_pairs={{0,2},{1,3},{2,0},{3,1},{4,6},{5,7},{6,4},{7,5},{8,10},{9,11},{10,... | collective-permute-start | bytes 2359304 | tf_op jit(solution)/shard_map/ppermute | solution.py:26
  974.5 32.4 %collective-permute-start.61 = (bf16[256,384]{1,0:T(8,128)(2,1)}, bf16[256,384]{1,0:T(8,128)(2,1)S(1)}, u32[]{:S(2)}, u32[]{:S(2)}) collective-permute-start(bf16[256,384]{1,0:T(8,128)(2,1)} %convolution_convert_fusion.41), channel_id=1, source_target_pairs={{4,0},{5,1},{6,2},{7,3},{12,8},{13,9},{14,10},{15,11},{20,16},{21,... | collective-permute-start | bytes 589832 | tf_op jit(solution)/shard_map/ppermute | solution.py:71
  1012.2 20.5 %collective-permute-start.63 = (bf16[512,768]{1,0:T(8,128)(2,1)S(1)}, bf16[512,768]{1,0:T(8,128)(2,1)S(1)}, u32[]{:S(2)}, u32[]{:S(2)}) collective-permute-start(bf16[512,768]{1,0:T(8,128)(2,1)S(1)} %pad_maximum_fusion.58), channel_id=1, source_target_pairs={{0,2},{1,3},{2,0},{3,1},{4,6},{5,7},{6,4},{7,5},{8,10},{9,11},{10,... | collective-permute-start | bytes 2359304 | tf_op jit(solution)/shard_map/ppermute | solution.py:26
  1014.6 32.4 %collective-permute-start.64 = (bf16[256,384]{1,0:T(8,128)(2,1)}, bf16[256,384]{1,0:T(8,128)(2,1)S(1)}, u32[]{:S(2)}, u32[]{:S(2)}) collective-permute-start(bf16[256,384]{1,0:T(8,128)(2,1)} %convolution_convert_fusion.40), channel_id=1, source_target_pairs={{4,0},{5,1},{6,2},{7,3},{12,8},{13,9},{14,10},{15,11},{20,16},{21,... | collective-permute-start | bytes 589832 | tf_op jit(solution)/shard_map/ppermute | solution.py:71
  1052.3 20.5 %collective-permute-start.66 = (bf16[512,768]{1,0:T(8,128)(2,1)S(1)}, bf16[512,768]{1,0:T(8,128)(2,1)S(1)}, u32[]{:S(2)}, u32[]{:S(2)}) collective-permute-start(bf16[512,768]{1,0:T(8,128)(2,1)S(1)} %pad_maximum_fusion.59), channel_id=1, source_target_pairs={{0,2},{1,3},{2,0},{3,1},{4,6},{5,7},{6,4},{7,5},{8,10},{9,11},{10,... | collective-permute-start | bytes 2359304 | tf_op jit(solution)/shard_map/ppermute | solution.py:26
  1054.7 32.4 %collective-permute-start.67 = (bf16[256,384]{1,0:T(8,128)(2,1)}, bf16[256,384]{1,0:T(8,128)(2,1)S(1)}, u32[]{:S(2)}, u32[]{:S(2)}) collective-permute-start(bf16[256,384]{1,0:T(8,128)(2,1)} %convolution_convert_fusion.39), channel_id=1, source_target_pairs={{4,0},{5,1},{6,2},{7,3},{12,8},{13,9},{14,10},{15,11},{20,16},{21,... | collective-permute-start | bytes 589832 | tf_op jit(solution)/shard_map/ppermute | solution.py:71
  1092.4 20.5 %collective-permute-start.69 = (bf16[512,768]{1,0:T(8,128)(2,1)S(1)}, bf16[512,768]{1,0:T(8,128)(2,1)S(1)}, u32[]{:S(2)}, u32[]{:S(2)}) collective-permute-start(bf16[512,768]{1,0:T(8,128)(2,1)S(1)} %pad_maximum_fusion.60), channel_id=1, source_target_pairs={{0,2},{1,3},{2,0},{3,1},{4,6},{5,7},{6,4},{7,5},{8,10},{9,11},{10,... | collective-permute-start | bytes 2359304 | tf_op jit(solution)/shard_map/ppermute | solution.py:26
  1094.9 32.3 %collective-permute-start.70 = (bf16[256,384]{1,0:T(8,128)(2,1)}, bf16[256,384]{1,0:T(8,128)(2,1)S(1)}, u32[]{:S(2)}, u32[]{:S(2)}) collective-permute-start(bf16[256,384]{1,0:T(8,128)(2,1)} %convolution_convert_fusion.38), channel_id=1, source_target_pairs={{4,0},{5,1},{6,2},{7,3},{12,8},{13,9},{14,10},{15,11},{20,16},{21,... | collective-permute-start | bytes 589832 | tf_op jit(solution)/shard_map/ppermute | solution.py:71
  1132.4 20.5 %collective-permute-start.72 = (bf16[512,768]{1,0:T(8,128)(2,1)S(1)}, bf16[512,768]{1,0:T(8,128)(2,1)S(1)}, u32[]{:S(2)}, u32[]{:S(2)}) collective-permute-start(bf16[512,768]{1,0:T(8,128)(2,1)S(1)} %pad_maximum_fusion.61), channel_id=1, source_target_pairs={{0,2},{1,3},{2,0},{3,1},{4,6},{5,7},{6,4},{7,5},{8,10},{9,11},{10,... | collective-permute-start | bytes 2359304 | tf_op jit(solution)/shard_map/ppermute | solution.py:26
  1134.9 32.4 %collective-permute-start.73 = (bf16[256,384]{1,0:T(8,128)(2,1)}, bf16[256,384]{1,0:T(8,128)(2,1)S(1)}, u32[]{:S(2)}, u32[]{:S(2)}) collective-permute-start(bf16[256,384]{1,0:T(8,128)(2,1)} %convolution_convert_fusion.37), channel_id=1, source_target_pairs={{4,0},{5,1},{6,2},{7,3},{12,8},{13,9},{14,10},{15,11},{20,16},{21,... | collective-permute-start | bytes 589832 | tf_op jit(solution)/shard_map/ppermute | solution.py:71
  1172.5 20.5 %collective-permute-start.75 = (bf16[512,768]{1,0:T(8,128)(2,1)S(1)}, bf16[512,768]{1,0:T(8,128)(2,1)S(1)}, u32[]{:S(2)}, u32[]{:S(2)}) collective-permute-start(bf16[512,768]{1,0:T(8,128)(2,1)S(1)} %pad_maximum_fusion.62), channel_id=1, source_target_pairs={{0,2},{1,3},{2,0},{3,1},{4,6},{5,7},{6,4},{7,5},{8,10},{9,11},{10,... | collective-permute-start | bytes 2359304 | tf_op jit(solution)/shard_map/ppermute | solution.py:26
  1174.9 32.4 %collective-permute-start.76 = (bf16[256,384]{1,0:T(8,128)(2,1)}, bf16[256,384]{1,0:T(8,128)(2,1)S(1)}, u32[]{:S(2)}, u32[]{:S(2)}) collective-permute-start(bf16[256,384]{1,0:T(8,128)(2,1)} %convolution_convert_fusion.36), channel_id=1, source_target_pairs={{4,0},{5,1},{6,2},{7,3},{12,8},{13,9},{14,10},{15,11},{20,16},{21,... | collective-permute-start | bytes 589832 | tf_op jit(solution)/shard_map/ppermute | solution.py:71
  1212.6 20.5 %collective-permute-start.78 = (bf16[512,768]{1,0:T(8,128)(2,1)S(1)}, bf16[512,768]{1,0:T(8,128)(2,1)S(1)}, u32[]{:S(2)}, u32[]{:S(2)}) collective-permute-start(bf16[512,768]{1,0:T(8,128)(2,1)S(1)} %pad_maximum_fusion.63), channel_id=1, source_target_pairs={{0,2},{1,3},{2,0},{3,1},{4,6},{5,7},{6,4},{7,5},{8,10},{9,11},{10,... | collective-permute-start | bytes 2359304 | tf_op jit(solution)/shard_map/ppermute | solution.py:26
  1215.0 32.4 %collective-permute-start.79 = (bf16[256,384]{1,0:T(8,128)(2,1)}, bf16[256,384]{1,0:T(8,128)(2,1)S(1)}, u32[]{:S(2)}, u32[]{:S(2)}) collective-permute-start(bf16[256,384]{1,0:T(8,128)(2,1)} %convolution_convert_fusion.35), channel_id=1, source_target_pairs={{4,0},{5,1},{6,2},{7,3},{12,8},{13,9},{14,10},{15,11},{20,16},{21,... | collective-permute-start | bytes 589832 | tf_op jit(solution)/shard_map/ppermute | solution.py:71
  1252.7 20.5 %collective-permute-start.81 = (bf16[512,768]{1,0:T(8,128)(2,1)S(1)}, bf16[512,768]{1,0:T(8,128)(2,1)S(1)}, u32[]{:S(2)}, u32[]{:S(2)}) collective-permute-start(bf16[512,768]{1,0:T(8,128)(2,1)S(1)} %pad_maximum_fusion.64), channel_id=1, source_target_pairs={{0,2},{1,3},{2,0},{3,1},{4,6},{5,7},{6,4},{7,5},{8,10},{9,11},{10,... | collective-permute-start | bytes 2359304 | tf_op jit(solution)/shard_map/ppermute | solution.py:26
  1255.1 32.4 %collective-permute-start.82 = (bf16[256,384]{1,0:T(8,128)(2,1)}, bf16[256,384]{1,0:T(8,128)(2,1)S(1)}, u32[]{:S(2)}, u32[]{:S(2)}) collective-permute-start(bf16[256,384]{1,0:T(8,128)(2,1)} %convolution_convert_fusion.34), channel_id=1, source_target_pairs={{4,0},{5,1},{6,2},{7,3},{12,8},{13,9},{14,10},{15,11},{20,16},{21,... | collective-permute-start | bytes 589832 | tf_op jit(solution)/shard_map/ppermute | solution.py:71
  (120 other events, 944.3 us)
where the time goes:
time: 1350 us; the launch traced here: 1340 us
  waiting for transfers between devices  624 us (46%)
  matrix products  547 us (41%)
  starting transfers between devices  71.4 us (5%)
  local copies, waits for them, and re-layouts  60.2 us (4%)
  other arithmetic  28.3 us (2%)
    ppermute x66, waiting for transfers between devices, gather_half(): lax.ppermute(gathered, 'group', partner_perm)  611 us
    dot_general x117, matrix products, mat_f32(): return jnp.dot(left_op, right_op, preferred_element_type=jnp.float32)  229 us
    sub x33, matrix products, transformer_block(): att_probs = jax.nn.softmax(scores, axis=-1).astype(jnp.bfloat16)  176 us
    dot_general x33, matrix products, transformer_block(): jnp.einsum('thd,hde->te', head_out, w_proj, preferred_element_type=jnp.fl...  142 us
    ppermute x17, starting transfers between devices, device_step(): res_recv = lax.ppermute(ctrl_res, 'group', to_base)  47.2 us
    slice x66, local copies, waits for them, and re-layouts, transformer_block(): key_heads = key_vals[:, :model_width].reshape(-1, head_count, head_dim)  32.7 us
  transfers between devices with their start and end apart: 86, of which 70 were waited for; matrix products, arithmetic and copies ran while one was open for 22% of the time, Pallas kernels for 0%

commit v1 on v0

v1 whole, which is shorter than its diff:
```python
import functools
import math

import jax
import jax.numpy as jnp
from jax import lax
from jax.experimental import pallas as pl
from jax.experimental.pallas import tpu as pltpu
from jax.sharding import PartitionSpec as P

EPS = 1e-6
MESH = pl.DeviceIdType.MESH
F32, BF16 = jnp.float32, jnp.bfloat16


def mat_f32(left_op, right_op):
    return jnp.dot(left_op, right_op, preferred_element_type=F32)


def mat_nt(left_op, right_op):
    return lax.dot_general(left_op, right_op, (((1,), (1,)), ((), ())), preferred_element_type=F32)


def norm_rows_of(values, gain, shift):
    wide = values.astype(F32)
    centered = wide - jnp.mean(wide, axis=-1, keepdims=True)
    variance = jnp.mean(centered * centered, axis=-1, keepdims=True)
    return (centered * lax.rsqrt(variance + EPS) * gain + shift).astype(BF16)


def gelu_tanh(v):
    k = math.sqrt(2.0 / math.pi)
    inner = v * (k + (k * 0.044715) * (v * v))
    half = 0.5 * v
    return half + half * jnp.tanh(inner)


def kernel(
    dims,
    x_ref, hint_ref, in_norm, out_norm, hint_proj, final_norm, w_out,
    in_qkv, in_proj, in_up, in_down, out_qkv, out_proj, out_up, out_down, zero_proj, skip_proj,
    y_ref,
    res, store, inbox, kv, qbuf, abuf, hbuf, s_buf, p_buf, l_buf, normf,
    wqkv, wproj, wup, wdown, wskip, zbuf, c0buf, ysend, yrecv,
    wsem, zsem, first_send, first_recv, kv_send, kv_recv, ctrl_send, box_recv, y_send, y_recv,
):
    group, n, slab, width, head_dim = dims
    n_in = n + 1
    slots = group // 2
    rows = slots * slab
    half = group // 2
    qc = rows // 2
    pair_w = 2 * head_dim
    pairs = width // pair_w
    scale = math.log2(math.e) * head_dim ** -0.5

    me = lax.axis_index("group")
    core = me % 2
    slot_me = me // 2
    base_dev = core
    ctrl_dev = half + core
    partner = me + 1 - 2 * core
    is_base = me < 2
    is_ctrl = (me >= half) & (me < half + 2)
    helper_of = 2 + 5 * core
    is_help = (me == 2) | (me == 7)
    help_core = (me == 7).astype(jnp.int32)
    branch = (me // half)

    def rcopy(src, dst, send, recv, dev):
        return pltpu.make_async_remote_copy(
            src_ref=src, dst_ref=dst, send_sem=send, recv_sem=recv, device_id={"group": dev}, device_id_type=MESH)

    barrier = pltpu.get_barrier_semaphore()
    for d in range(1, group):
        pl.semaphore_signal(barrier, inc=1, device_id={"group": (me + d) % group}, device_id_type=MESH)
    pl.semaphore_wait(barrier, group - 1)

    def w_copies(src5, idx, slot):
        out = []
        for k, (s, d) in enumerate(zip(src5, (wqkv, wproj, wup, wdown))):
            out.append(pltpu.make_async_copy(s.at[idx], d.at[slot], wsem.at[slot, k]))
        return out

    ins = (in_qkv, in_proj, in_up, in_down)
    outs = (out_qkv, out_proj, out_up, out_down)

    @pl.when(is_base | is_ctrl)
    def _():
        for c in w_copies(ins, (branch, 0), 0):
            c.start()

    slab_rows = pl.ds(pl.multiple_of(slot_me * slab, slab), slab)
    to_base = rcopy(x_ref, res.at[slab_rows], first_send.at[0], first_recv.at[slot_me], base_dev)

    @pl.when(jnp.logical_not(is_base))
    def _():
        to_base.start()

    c0buf[...] = (x_ref[...].astype(F32) + mat_f32(hint_ref[...], hint_proj[...])).astype(BF16)
    to_ctrl = rcopy(c0buf, res.at[slab_rows], first_send.at[1], first_recv.at[slot_me], ctrl_dev)

    @pl.when(jnp.logical_not(is_ctrl))
    def _():
        to_ctrl.start()

    @pl.when(is_base)
    def _():
        res[slab_rows, :] = x_ref[...]

    @pl.when(is_ctrl)
    def _():
        res[slab_rows, :] = c0buf[...]

    @pl.when(is_base | is_ctrl)
    def _():
        for s in range(slots):
            @pl.when(s != slot_me)
            def _():
                blk = res.at[pl.ds(s * slab, slab)]
                rcopy(blk, blk, first_send.at[0], first_recv.at[s], me).wait_recv()

    def block(i):
        slot = i % 2

        @pl.when(i < n_in)
        def _():
            normf[...] = in_norm[branch, jnp.minimum(i, n_in - 1)].astype(F32)

        @pl.when(i >= n_in)
        def _():
            normf[...] = out_norm[jnp.maximum(i - n_in, 0)].astype(F32)

        g1, b1, g2, b2 = (normf[k:k + 1, :] for k in range(4))
        cps = w_copies(ins, (0, 0), slot)
        cps[0].wait()
        sends = []
        for c in range(2):
            r = slice(c * qc, (c + 1) * qc)
            t = norm_rows_of(res[r, :], g1, b1)
            kv[slot, r, :] = mat_f32(t, wqkv[slot, :, width:]).astype(BF16)
            cp = rcopy(kv.at[slot, pl.ds(c * qc, qc)], kv.at[slot, pl.ds(rows + c * qc, qc)],
                       kv_send.at[slot, c], kv_recv.at[slot, c], partner)
            cp.start()
            sends.append(cp)
            qbuf[r, :] = mat_f32(t, wqkv[slot, :, :width]).astype(BF16)
        for cp in sends:
            cp.wait_recv()
        low = lax.broadcasted_iota(jnp.int32, (qc, pair_w), 1) < head_dim
        unit = 0
        for c in range(2):
            r = slice(c * qc, (c + 1) * qc)
            for p in range(pairs):
                b = unit % 2
                unit += 1
                cols = slice(p * pair_w, (p + 1) * pair_w)
                vcols = slice(width + p * pair_w, width + (p + 1) * pair_w)
                q = qbuf[r, cols]
                zero = jnp.zeros_like(q)
                both = jnp.concatenate([jnp.where(low, q, zero), jnp.where(low, zero, q)], axis=0)
                s_buf[b] = mat_nt(both, kv[slot, :, cols])
                step = 64
                for rb in range(0, 2 * qc, step):
                    s = s_buf[b, rb:rb + step, :]
                    m = jnp.max(s, axis=-1, keepdims=True)
                    e = jnp.exp2((s - m) * scale)
                    l = jnp.sum(e, axis=-1, keepdims=True)
                    p_buf[b, rb:rb + step, :] = e.astype(BF16)
                    l_buf[b, rb:rb + step, :] = jnp.broadcast_to(1.0 / l, (step, pair_w))
                o = mat_f32(p_buf[b], kv[slot, :, vcols]) * l_buf[b]
                abuf[r, cols] = jnp.where(low, o[:qc], o[qc:]).astype(BF16)
        for k in range(1, 4):
            cps[k].wait()
        for c in range(2):
            r = slice(c * qc, (c + 1) * qc)
            u = (res[r, :].astype(F32) + mat_f32(abuf[r, :], wproj[slot])).astype(BF16)
            t = norm_rows_of(u, g2, b2)
            hbuf[...] = gelu_tanh(mat_f32(t, wup[slot])).astype(BF16)
            res[r, :] = (u.astype(F32) + mat_f32(hbuf[...], wdown[slot])).astype(BF16)
        for cp in sends:
            cp.wait_send()

    n_iter = jnp.where(is_base, n_in + n, n_in)

    def c_send(i):
        return rcopy(store.at[i], inbox.at[i], ctrl_send.at[i], box_recv.at[i], helper_of)

    def box_wait(i):
        rcopy(inbox.at[i], inbox.at[i], ctrl_send.at[i], box_recv.at[i], me).wait_recv()

    def layer(i, carry):
        nxt = i + 1

        @pl.when(nxt < n_in)
        def _():
            for c in w_copies(ins, (branch, jnp.minimum(nxt, n_in - 1)), nxt % 2):
                c.start()

        @pl.when((nxt >= n_in) & (nxt < n_iter))
        def _():
            j = jnp.clip(nxt - n_in, 0, n - 1)
            for c in w_copies(outs, j, nxt % 2):
                c.start()
            pltpu.make_async_copy(skip_proj.at[j], wskip.at[nxt % 2], wsem.at[nxt % 2, 4]).start()

        @pl.when(i == n_in)
        def _():
            box_wait(n)
            res[...] = (res[...].astype(F32) + inbox[n].astype(F32)).astype(BF16)

        @pl.when(i >= n_in)
        def _():
            src = jnp.clip(n - 1 - (i - n_in), 0, n - 1)
            box_wait(src)
            slot = i % 2
            pltpu.make_async_copy(skip_proj.at[0], wskip.at[slot], wsem.at[slot, 4]).wait()
            for c in range(2):
                r = slice(c * qc, (c + 1) * qc)
                sk = (store[src, r, :].astype(F32) + inbox[src, r, :].astype(F32)).astype(BF16)
                top = mat_f32(res[r, :], wskip[slot, :width, :])
                res[r, :] = (top + mat_f32(sk, wskip[slot, width:, :])).astype(BF16)

        block(i)

        @pl.when(i < n_in)
        def _():
            ii = jnp.minimum(i, n)
            store[ii] = res[...]

            @pl.when(is_ctrl)
            def _():
                c_send(ii).start()

        return carry

    @pl.when(is_base | is_ctrl)
    def _():
        lax.fori_loop(0, n_iter, layer, 0)

    @pl.when(is_ctrl)
    def _():
        lax.fori_loop(0, n_in, lambda i, a: (c_send(i).wait_send(), a)[1], 0)

    @pl.when(is_help)
    def _():
        def z_copy(i):
            return pltpu.make_async_copy(zero_proj.at[i], zbuf.at[i % 2], zsem.at[i % 2])

        def r_send(i):
            return rcopy(store.at[i], inbox.at[i], ctrl_send.at[i], box_recv.at[i], help_core)

        z_copy(0).start()

        def step(i, a):
            @pl.when(i + 1 < n_in)
            def _():
                z_copy(jnp.minimum(i + 1, n)).start()

            z_copy(i).wait()
            box_wait(i)
            for c in range(2):
                r = slice(c * qc, (c + 1) * qc)
                store[i, r, :] = mat_f32(inbox[i, r, :], zbuf[i % 2]).astype(BF16)
            r_send(i).start()
            return a

        lax.fori_loop(0, n_in, step, 0)
        lax.fori_loop(0, n_in, lambda i, a: (r_send(i).wait_send(), a)[1], 0)

    @pl.when(is_base)
    def _():
        gf, bf = final_norm[0:1, :].astype(F32), final_norm[1:2, :].astype(F32)
        copies = []
        for s in range(slots):
            t = norm_rows_of(res[s * slab:(s + 1) * slab, :], gf, bf)
            y = mat_f32(t, w_out[...]).astype(BF16)
            if s == 0:
                y_ref[...] = y
            else:
                ysend[s] = y
                cp = rcopy(ysend.at[s], yrecv, y_send.at[s], y_recv, 2 * s + core)
                cp.start()
                copies.append(cp)
        for cp in copies:
            cp.wait_send()

    @pl.when(jnp.logical_not(is_base))
    def _():
        to_base.wait_send()
        rcopy(yrecv, yrecv, y_send.at[0], y_recv, me).wait_recv()
        y_ref[...] = yrecv[...]

    @pl.when(jnp.logical_not(is_ctrl))
    def _():
        to_ctrl.wait_send()


def solution(mesh):
    group = mesh.shape["group"]

    def device_step(x_own, hint_own, in_qkv, in_proj, in_up, in_down, in_norm, out_qkv, out_proj, out_up, out_down, out_norm, zero_proj, hint_proj, skip_proj, final_norm, w_out):
        slab, width = x_own.shape
        n = skip_proj.shape[0]
        heads, head_dim = in_proj.shape[2], in_proj.shape[3]
        hidden = in_up.shape[-1]
        rows = (group // 2) * slab
        qc = rows // 2
        in_proj = in_proj.reshape(in_proj.shape[:2] + (width, width))
        out_proj = out_proj.reshape(out_proj.shape[:1] + (width, width))
        vm = pl.BlockSpec(memory_space=pltpu.VMEM)
        hb = pl.BlockSpec(memory_space=pl.ANY)
        dma = pltpu.SemaphoreType.DMA
        return pl.pallas_call(
            functools.partial(kernel, (group, n, slab, width, head_dim)),
            out_shape=jax.ShapeDtypeStruct((slab, width), BF16),
            in_specs=[vm] * 7 + [hb] * 10,
            out_specs=vm,
            scratch_shapes=[
                pltpu.VMEM((rows, width), BF16),
                pltpu.VMEM((n + 1, rows, width), BF16),
                pltpu.VMEM((n + 1, rows, width), BF16),
                pltpu.VMEM((2, 2 * rows, 2 * width), BF16),
                pltpu.VMEM((rows, width), BF16),
                pltpu.VMEM((rows, width), BF16),
                pltpu.VMEM((qc, hidden), BF16),
                pltpu.VMEM((2, 2 * qc, 2 * rows), F32),
                pltpu.VMEM((2, 2 * qc, 2 * rows), BF16),
                pltpu.VMEM((2, 2 * qc, 2 * head_dim), F32),
                pltpu.VMEM((4, width), F32),
                pltpu.VMEM((2, width, 3 * width), BF16),
                pltpu.VMEM((2, width, width), BF16),
                pltpu.VMEM((2, width, hidden), BF16),
                pltpu.VMEM((2, hidden, width), BF16),
                pltpu.VMEM((2, 2 * width, width), BF16),
                pltpu.VMEM((2, width, width), BF16),
                pltpu.VMEM((slab, width), BF16),
                pltpu.VMEM((group // 2, slab, width), BF16),
                pltpu.VMEM((slab, width), BF16),
                dma((2, 5)), dma((2,)),
                dma((2,)), dma((group // 2,)),
                dma((2, 2)), dma((2, 2)),
                dma((n + 1,)), dma((n + 1,)),
                dma((group // 2,)), dma,
            ],
            compiler_params=pltpu.CompilerParams(
                collective_id=0, has_side_effects=True, vmem_limit_bytes=60 * 1024 * 1024),
        )(x_own, hint_own, in_norm, out_norm, hint_proj, final_norm, w_out,
          in_qkv, in_proj, in_up, in_down, out_qkv, out_proj, out_up, out_down, zero_proj, skip_proj)

    tok_spec = P(("data", "group"), None)
    return jax.shard_map(device_step, mesh=mesh, in_specs=(tok_spec, tok_spec) + (P(),) * 15, out_specs=tok_spec, check_vma=False)
```

time: 1350 us -> 373 us (0.28)
  waiting for transfers between devices: 624 us -> 0 us
  matrix products: 547 us -> 0 us
  Pallas kernels: 0 us -> 369 us
  starting transfers between devices: 71.4 us -> 0 us
  local copies, waits for them, and re-layouts: 60.2 us -> 1.54 us
  other arithmetic: 28.3 us -> 0 us
    ppermute x86 -> x0, waiting for transfers between devices: 624 us -> none  [the longest x66 611 us: gather_half(): lax.ppermute(gathered, 'group', partner_perm)]
    dot_general x150 -> x0, matrix products: 371 us -> none  [the longest x117 229 us: mat_f32(): return jnp.dot(left_op, right_op, preferred_element_type=jnp.float32)]
    pallas_call x0 -> x1, Pallas kernels: none -> 369 us  [device_step(): pl.pallas_call(functools.partial(kernel, (group, n, slab, width, head_dim...]
    sub x33 -> x0, matrix products: 176 us -> none  [transformer_block(): att_probs = jax.nn.softmax(scores, axis=-1).astype(jnp.bfloat16)]
    ppermute x86 -> x0, starting transfers between devices: 71.4 us -> none  [the longest x17 47.2 us: device_step(): res_recv = lax.ppermute(ctrl_res, 'group', to_base)]
    slice x199 -> x0, local copies, waits for them, and re-layouts: 58 us -> none  [the longest x66 32.7 us: transformer_block(): key_heads = key_vals[:, :model_width].reshape(-1, head_count, head_dim)]
  transfers between devices with their start and end apart: 86 -> 0, of which waited for: 70 -> 0; matrix products, arithmetic and copies ran while one was open for 22% -> 0% of each run, Pallas kernels for 0% -> 0%
where the time goes in v1:
time: 373 us; the launch traced here: 371 us
  Pallas kernels  369 us (99%)
    pallas_call x1, Pallas kernels, device_step(): pl.pallas_call(functools.partial(kernel, (group, n, slab, width, head_dim...  369 us

profile of v1, /device:TPU:86, one launch (start us, length us, event | category | flops | bytes accessed | tf_op | source)
XLA Modules:
  0.0 370.7 jit_solution(10030767715589044561)
XLA Ops:
  0.0 369.1 %shard_map.163 = bf16[128,384]{1,0:T(8,128)(2,1)} custom-call(bf16[128,384]{1,0:T(8,128)(2,1)} %x_ref.1, bf16[128,384]{1,0:T(8,128)(2,1)} %hint_ref.1, bf16[2,17,4,384]{3,2,1,0:T(4,128)(2,1)} %in_norm.1, bf16[16,4,384]{2,1,0:T(4,128)(2,1)} %out_norm.1, bf16[384,384]{1,0:T(8,128)(2,1)} %hint_proj.1, bf16[2,384]{1,0:T(2,128)(2,1)} %final_norm.1, ...), custom_call_target="tpu_custom_call" | custom-call | tf_op jit(solution)/shard_map/pallas_call | solution.py:313
  369.2 1.5 copy.19
